TPU v7x, 32 devices: a whole 2x2x4 slice. The times are simulated.
32 devices in a mesh: grp: 4 (over y, core), sub: 8 (over z, x).
Axes of the slice: x: 2, y: 2, z: 4, core: 2. Of those that a mesh axis runs over, the one named last changes fastest.
Arguments:
- fields: float32 [4, 35, 8192], P(None, None, ('grp', 'sub')), may hold values from -6 to 6
- section_store: float32 [4, 35, 8192], P(None, None, ('grp', 'sub')), may hold values from -6 to 6
- metric_terms: float32 [9, 8192], P(None, ('grp', 'sub')), may hold values from -6 to 6
- normals: float32 [4, 3, 8192], P(None, None, ('grp', 'sub')), may hold values from -3 to 3
- face_scale: float32 [4, 8192], P(None, ('grp', 'sub')), may hold values from 1 to 4
- damping: float32 [8192], P(('grp', 'sub')), may hold values from 1 to 10
- absorb_mask: int32 [8192], P(('grp', 'sub')), may hold values from 0 to 1
- refine_level: int32 [8192], P(('grp', 'sub')), may hold values from 0 to 2
- face_source: int32 [4, 8192], P(None, ('grp', 'sub')), may hold values from -1 to 1343, as said below
- orientation: int32 [4, 8192], P(None, ('grp', 'sub')), may hold values from 0 to 5, as said below
- derivative: float32 [3, 35, 35], replicated, may hold values from -1 to 1
- lift_matrix: float32 [35, 60], replicated, may hold values from -0.75 to 0.75
Outputs:
- fields_next: float32 [4, 35, 8192], P(None, None, ('grp', 'sub'))
- store_next: float32 [4, 35, 8192], P(None, None, ('grp', 'sub'))
- absorbed_energy: float32 [], replicated
Inputs may be any that keep to these rules, and one draw needn't show every extreme that they name: `face_source`: A device uses the slots of a block from rank 0 on without gaps; it never uses block s (its own sub index), nor block 8 at the first grp index or block 9 at the last. For a sub peer b with |b - s| <= 4 at most 32 ranks are used, for other peers at most 8, and across grp at most 32; in every draw some near pair uses all 32, some farther pair all 8, and some pair across grp all 32. Local neighbours lie on the same device. `orientation`: paired faces have inverse orientations: 1 and 2 swap, 0, 3, 4 and 5 stay.
All inputs are finite; a program needn't handle non-finite values.
Results may differ from a plain program's by a relative error of at most 0.0003.
Values sent between devices are 32-bit elements; how exact they have to be, the bound alone decides.
A program may use at most 64 MiB of HBM per device.

v0:
```python
import functools

import jax
import jax.numpy as jnp
import numpy as np
from jax import lax
from jax.experimental import pallas as pl
from jax.experimental.pallas import tpu as pltpu
from jax.sharding import PartitionSpec as P

VOLUME_NODES = 35
FACE_NODES = 15
NEAR_PEERS = 4
NODE_PAD = 48
SLOPE_PAD = 40
ROWS = 64

RUNGE_CARRY = -567301805773.0 / 1357537059087.0
RUNGE_ADVANCE = 5161836677717.0 / 13612068292357.0
TIME_STEP = 0.02
OPERANDS = 13
MESH = pl.DeviceIdType.MESH


def node_tables():
    volume_list = [
        (a, b, c, 4 - a - b - c) for a in range(5) for b in range(5 - a) for c in range(5 - a - b)
    ]
    triples = [(a, b, 4 - a - b) for a in range(5) for b in range(5 - a)]
    face_index = np.zeros((4, 15), np.int32)
    for facet in range(4):
        others = [corner for corner in range(4) if corner != facet]
        for node_pos in range(15):
            corners = [0, 0, 0, 0]
            for place_pos in range(3):
                corners[others[place_pos]] = triples[node_pos][place_pos]
            face_index[facet, node_pos] = volume_list.index(tuple(corners))
    vertex_orders = [(0, 1, 2), (1, 2, 0), (2, 0, 1), (0, 2, 1), (2, 1, 0), (1, 0, 2)]
    turn_index = np.zeros((6, 15), np.int32)
    for option in range(6):
        q = vertex_orders[option]
        for node_pos in range(15):
            t = triples[node_pos]
            turn_index[option, node_pos] = triples.index((t[q[0]], t[q[1]], t[q[2]]))
    return face_index, turn_index


def constant_table():
    face_index, turn_index = node_tables()
    table = np.zeros((ROWS, 1024), np.float32)
    for f in range(4):
        for j in range(15):
            table[f * 16 + j, face_index[f, j]] = 1.0
            table[f * 15 + j, 896 + f * 16 + j] = 1.0
    for part in range(2):
        for o in range(6):
            for c in range(4):
                for j in range(15):
                    col = 128 + part * 384 + o * 64 + c * 16 + turn_index[o, j]
                    table[c * 16 + j, col] = 1.0
    return jnp.asarray(table, jnp.bfloat16)


def split(value):
    high = value.astype(jnp.bfloat16)
    low = (value - high.astype(jnp.float32)).astype(jnp.bfloat16)
    return high, low


def dot(left, right):
    return jnp.dot(left, right, preferred_element_type=jnp.float32)


def dot3(left, right):
    (lh, ll), (rh, rl) = left, right
    return dot(lh, rh) + (dot(lh, rl) + dot(ll, rh))


def flat_row(ref_rows):
    return jnp.concatenate(ref_rows, axis=1)


def kernel(
    n_grp,
    n_sub,
    direct,
    *refs,
):
    operands, rest = refs[:OPERANDS], refs[OPERANDS:]
    results, rest = rest[:4], rest[4:]
    copies, rest = results[:2] + rest[: OPERANDS - 2], rest[OPERANDS - 2 :]
    body(n_grp, n_sub, direct, operands, *copies, *results[2:], *rest)


def body(
    n_grp,
    n_sub,
    direct,
    operands,
    fields,
    store,
    metric,
    normals,
    face_scale,
    damping,
    mask,
    level,
    source,
    orient,
    derivative,
    lift,
    table,
    change_out,
    energy_out,
    fpad,
    dpad,
    lpad,
    outbox,
    inbox,
    base,
    energy_row,
    energy_mid,
    energy_a,
    energy_b,
    send_sem,
    recv_sem,
    esend_a,
    erecv_a,
    esend_b,
    erecv_b,
    load_sem,
):
    copies = (
        fields,
        store,
        metric,
        normals,
        face_scale,
        damping,
        mask,
        level,
        source,
        orient,
        derivative,
        lift,
        table,
    )
    loads = [
        pltpu.make_async_copy(operands[i], copies[i], load_sem.at[i]) for i in range(OPERANDS)
    ]
    early = (0, 8, 12)
    elements = face_scale.shape[1]
    tiles = elements // 128
    faces = 4 * elements
    half = elements // 16
    n_blocks = n_sub + 2

    def node_rows(c, t):
        return pl.ds(t * 4 + c, VOLUME_NODES, stride=4 * tiles)

    def read(ref, c):
        return jnp.concatenate([ref[node_rows(c, t), :] for t in range(tiles)], axis=1)

    def write(ref, c, value):
        for t in range(tiles):
            ref[node_rows(c, t), :] = value[:, t * 128 : (t + 1) * 128]

    g = lax.axis_index("grp")
    s = lax.axis_index("sub")
    inbox[...] = jnp.zeros_like(inbox)

    def sub_peer(k):
        return lax.rem(s + k, n_sub)

    def grp_peer(k):
        return lax.rem(g + k, n_grp)

    barrier = pltpu.get_barrier_semaphore()
    greeted = 0
    for kg in range(n_grp):
        for ks in range(n_sub):
            if (kg, ks) == (0, 0) or not (direct or kg == 0 or ks == 0):
                continue
            pl.semaphore_signal(
                barrier, inc=1, device_id=(grp_peer(kg), sub_peer(ks)), device_id_type=MESH
            )
            greeted += 1
    for i in early:
        loads[i].start()
    for i in range(OPERANDS):
        if i not in early:
            loads[i].start()
    for i in early:
        loads[i].wait()

    fpad[VOLUME_NODES:, :] = jnp.zeros((NODE_PAD - VOLUME_NODES, faces), jnp.float32)
    for c in range(4):
        fpad[0:VOLUME_NODES, c * elements : (c + 1) * elements] = read(fields, c)
    field_parts = split(fpad[...])
    pick = table[:, 0:NODE_PAD]

    def by_face(value):
        return jnp.concatenate(
            [
                jnp.concatenate(
                    [
                        value[f * 16 : (f + 1) * 16, c * elements : (c + 1) * elements]
                        for c in range(4)
                    ],
                    axis=0,
                )
                for f in range(4)
            ],
            axis=1,
        )

    inner_high = by_face(dot(pick, field_parts[0]))
    inner_low = by_face(dot(pick, field_parts[1]))
    codes = flat_row([source[f : f + 1, :] for f in range(4)])
    high_b = inner_high.astype(jnp.bfloat16)
    low_b = inner_low.astype(jnp.bfloat16)

    def slots_hot(part):
        row = lax.broadcasted_iota(jnp.int32, (n_blocks * half, faces), 0)
        slot = (row // half) * (2 * half) + part * half + row % half
        return jnp.where(slot == codes - faces, 1.0, 0.0).astype(jnp.bfloat16)

    hot = [slots_hot(0), slots_hot(1)]
    nothing = jnp.zeros_like(high_b)
    packed = None
    for part in range(2):
        for value in (high_b, low_b):
            weights = jnp.concatenate([value, nothing] if part == 0 else [nothing, value], axis=0)
            term = lax.dot_general(
                hot[part], weights, (((1,), (1,)), ((), ())), preferred_element_type=jnp.float32
            )
            packed = term if packed is None else packed + term
    outbox[...] = packed.reshape(n_blocks, half, 2 * ROWS)

    pl.semaphore_wait(barrier, greeted)

    def sub_copy(k, rows):
        peer = sub_peer(k)
        return pltpu.make_async_remote_copy(
            src_ref=outbox.at[peer, pl.ds(0, rows)],
            dst_ref=inbox.at[s, pl.ds(0, rows)],
            send_sem=send_sem.at[peer],
            recv_sem=recv_sem.at[s],
            device_id=(g, peer),
            device_id_type=MESH,
        )

    def sub_arrival(k, rows):
        peer = sub_peer(k)
        return pltpu.make_async_remote_copy(
            src_ref=outbox.at[peer, pl.ds(0, rows)],
            dst_ref=inbox.at[peer, pl.ds(0, rows)],
            send_sem=send_sem.at[peer],
            recv_sem=recv_sem.at[peer],
            device_id=(g, peer),
            device_id_type=MESH,
        )

    def grp_copy(up):
        block, landing = (n_sub + 1, n_sub) if up else (n_sub, n_sub + 1)
        peer = jnp.minimum(g + 1, n_grp - 1) if up else jnp.maximum(g - 1, 0)
        return pltpu.make_async_remote_copy(
            src_ref=outbox.at[block],
            dst_ref=inbox.at[landing],
            send_sem=send_sem.at[block],
            recv_sem=recv_sem.at[landing],
            device_id=(peer, s),
            device_id_type=MESH,
        )

    def each_sub(make, act):
        for k in range(1, n_sub):
            gap = jnp.abs(sub_peer(k) - s)

            @pl.when(gap <= NEAR_PEERS)
            def _():
                act(make(k, half))

            @pl.when(gap > NEAR_PEERS)
            def _():
                act(make(k, half // 2))

    each_sub(sub_copy, lambda copy: copy.start())

    @pl.when(g > 0)
    def _():
        grp_copy(False).start()

    @pl.when(g < n_grp - 1)
    def _():
        grp_copy(True).start()

    for i in range(OPERANDS):
        if i not in early:
            loads[i].wait()
    growth = jnp.exp2(level[...].astype(jnp.float32))
    absorb = damping[...] * mask[...].astype(jnp.float32)
    dpad[...] = jnp.zeros_like(dpad)
    for d in range(3):
        dpad[d * SLOPE_PAD : d * SLOPE_PAD + VOLUME_NODES, 0:VOLUME_NODES] = derivative[d]
    slopes = dot3(split(dpad[...]), field_parts)

    def slope(d, c):
        return slopes[
            d * SLOPE_PAD : (d + 1) * SLOPE_PAD, c * elements : (c + 1) * elements
        ]

    def field(c):
        return fpad[0:VOLUME_NODES, c * elements : (c + 1) * elements]

    scaled = metric[...] * growth
    for c in range(4):
        total = None
        for x in range(3) if c == 0 else (c - 1,):
            for y in range(3):
                term = scaled[3 * x + y : 3 * x + y + 1, :] * slope(y, x + 1 if c == 0 else 0)
                total = term if total is None else total + term
        change = -total[0:VOLUME_NODES] - absorb * field(c)
        base[c, 0:VOLUME_NODES, :] = change

    lpad[...] = jnp.zeros_like(lpad)
    lpad[0:VOLUME_NODES, 0:60] = lift[...]
    spread = table[:, 896:960]
    lift_parts = tuple(dot(part, spread).astype(jnp.bfloat16) for part in split(lpad[...]))

    stacked = jnp.concatenate([high_b, low_b], axis=0)
    gathered = None
    for f in range(4):
        row = lax.broadcasted_iota(jnp.int32, (elements, faces), 0) + f * elements
        chosen = jnp.where(row == codes, 1.0, 0.0).astype(jnp.bfloat16)
        term = dot(stacked[:, f * elements : (f + 1) * elements], chosen)
        gathered = term if gathered is None else gathered + term

    each_sub(sub_arrival, lambda copy: copy.wait_recv())

    @pl.when(g > 0)
    def _():
        grp_copy(True).wait_recv()

    @pl.when(g < n_grp - 1)
    def _():
        grp_copy(False).wait_recv()

    arrived = inbox[...].reshape(n_blocks * half, 2 * ROWS).T
    for part in range(2):
        pieces = split(arrived[part * ROWS : (part + 1) * ROWS])
        gathered = gathered + dot(jnp.concatenate(pieces, axis=0), hot[part])

    turns = flat_row([orient[f : f + 1, :] for f in range(4)])
    pieces = []
    for part in range(2):
        value = gathered[part * ROWS : (part + 1) * ROWS]
        for o in range(6):
            pieces.append(jnp.where(turns == o, value, 0.0).astype(jnp.bfloat16))
    outside = dot(table[:, 128:896], jnp.concatenate(pieces, axis=0))
    inside = inner_high + inner_low

    wall = codes < 0
    normal = [
        flat_row([normals[x, f : f + 1, :] for f in range(4)]) for x in range(3)
    ]
    weight = 0.5 * flat_row([face_scale[f : f + 1, :] * growth for f in range(4)])
    press = jnp.where(wall, 0.0, inside[0:16] - outside[0:16])
    normal_in = None
    for x in range(3):
        term = normal[x] * inside[16 * (x + 1) : 16 * (x + 2)]
        normal_in = term if normal_in is None else normal_in + term
    normal_jump = None
    for x in range(3):
        rows = slice(16 * (x + 1), 16 * (x + 2))
        jump = jnp.where(wall, 2.0 * normal[x] * normal_in, inside[rows] - outside[rows])
        term = normal[x] * jump
        normal_jump = term if normal_jump is None else normal_jump + term
    flux_press = weight * (normal_jump - press)
    fluxes = [flux_press] + [-normal[x] * flux_press for x in range(3)]
    flux = jnp.concatenate(
        [
            jnp.concatenate(
                [flux_c[:, f * elements : (f + 1) * elements] for f in range(4)], axis=0
            )
            for flux_c in fluxes
        ],
        axis=1,
    )
    lifted = dot3(lift_parts, split(flux))
    squares = None
    changes = []
    for c in range(4):
        lift_c = lifted[0:VOLUME_NODES, c * elements : (c + 1) * elements]
        change = base[c, 0:VOLUME_NODES, :] + lift_c
        stored = RUNGE_CARRY * read(store, c) + TIME_STEP * change
        changes.append(change)
        moved = field(c) + RUNGE_ADVANCE * stored
        squares = moved * moved if squares is None else squares + moved * moved
    weighted = absorb * jnp.sum(squares, axis=0, keepdims=True)
    partial = weighted[:, 0:128]
    for at in range(128, elements, 128):
        partial = partial + weighted[:, at : at + 128]
    energy_row[...] = partial

    def write_changes():
        for c in range(4):
            write(change_out, c, TIME_STEP * changes[c])

    def spread_rows(source_row, landing, sent, got, mine, peers, after_sends=lambda: None):
        def copy(peer, device, slot):
            return pltpu.make_async_remote_copy(
                src_ref=source_row,
                dst_ref=landing.at[slot],
                send_sem=sent.at[peer],
                recv_sem=got.at[slot],
                device_id=device,
                device_id_type=MESH,
            )

        for peer, device in peers:
            copy(peer, device, mine).start()
        landing[mine] = source_row[...]
        after_sends()
        for peer, device in peers:
            copy(peer, device, peer).wait_recv()
        for peer, device in peers:
            copy(peer, device, mine).wait_send()
        return jnp.sum(landing[...], axis=0)

    if direct:
        everyone = [
            (grp_peer(kg) * n_sub + sub_peer(ks), (grp_peer(kg), sub_peer(ks)))
            for kg in range(n_grp)
            for ks in range(n_sub)
            if (kg, ks) != (0, 0)
        ]
        total = spread_rows(energy_row, energy_a, esend_a, erecv_a, g * n_sub + s, everyone, write_changes)
    else:
        row_peers = [(sub_peer(k), (g, sub_peer(k))) for k in range(1, n_sub)]
        energy_mid[...] = spread_rows(
            energy_row, energy_a, esend_a, erecv_a, s, row_peers, write_changes
        )
        column_peers = [(grp_peer(k), (grp_peer(k), s)) for k in range(1, n_grp)]
        total = spread_rows(energy_mid, energy_b, esend_b, erecv_b, g, column_peers)
    divisor = elements * n_grp * n_sub * VOLUME_NODES
    energy_out[0, 0] = jnp.sum(total) / divisor

    each_sub(sub_copy, lambda copy: copy.wait_send())

    @pl.when(g > 0)
    def _():
        grp_copy(False).wait_send()

    @pl.when(g < n_grp - 1)
    def _():
        grp_copy(True).wait_send()


def local(
    fields,
    section_store,
    metric_terms,
    normals,
    face_scale,
    damping,
    absorb_mask,
    refine_level,
    face_source,
    orientation,
    derivative,
    lift_matrix,
):
    elements = fields.shape[2]
    n_grp, n_sub = lax.axis_size("grp"), lax.axis_size("sub")
    direct = n_grp * n_sub <= 64
    n_blocks = n_sub + 2
    half = elements // 16
    slots_a = n_grp * n_sub if direct else n_sub
    row = lambda value: value.reshape(1, elements)
    vmem = pl.BlockSpec(memory_space=pltpu.VMEM)
    f32 = jnp.float32
    tiles = elements // 128

    def to_rows(value):
        value = value.transpose(1, 0, 2).reshape(VOLUME_NODES, 4, tiles, 128)
        return value.transpose(0, 2, 1, 3).reshape(VOLUME_NODES * tiles * 4, 128)

    def from_rows(value):
        value = value.reshape(VOLUME_NODES, tiles, 4, 128).transpose(0, 2, 1, 3)
        return value.reshape(VOLUME_NODES, 4, elements).transpose(1, 0, 2)

    flat = (VOLUME_NODES * tiles * 4, 128)
    arguments = (
        to_rows(fields),
        to_rows(section_store),
        metric_terms,
        normals.transpose(1, 0, 2),
        face_scale,
        row(damping),
        row(absorb_mask),
        row(refine_level),
        face_source,
        orientation,
        derivative,
        lift_matrix,
        constant_table(),
    )
    held_fields, held_store, stepped, energy = pl.pallas_call(
        functools.partial(kernel, n_grp, n_sub, direct),
        out_shape=(
            pltpu.VMEM(flat, f32),
            pltpu.VMEM(flat, f32),
            pltpu.VMEM(flat, f32),
            jax.ShapeDtypeStruct((1, 1), f32),
        ),
        in_specs=[pl.BlockSpec(memory_space=pl.ANY)] * OPERANDS,
        out_specs=(vmem, vmem, vmem, pl.BlockSpec(memory_space=pltpu.SMEM)),
        scratch_shapes=[pltpu.VMEM(value.shape, value.dtype) for value in arguments[2:]]
        + [
            pltpu.VMEM((NODE_PAD, 4 * elements), f32),
            pltpu.VMEM((3 * SLOPE_PAD, NODE_PAD), f32),
            pltpu.VMEM((SLOPE_PAD, ROWS), f32),
            pltpu.VMEM((n_blocks, half, 2 * ROWS), f32),
            pltpu.VMEM((n_blocks, half, 2 * ROWS), f32),
            pltpu.VMEM((4, SLOPE_PAD, elements), f32),
            pltpu.VMEM((1, 128), f32),
            pltpu.VMEM((1, 128), f32),
            pltpu.VMEM((slots_a, 1, 128), f32),
            pltpu.VMEM((n_grp, 1, 128), f32),
            pltpu.SemaphoreType.DMA((n_blocks,)),
            pltpu.SemaphoreType.DMA((n_blocks,)),
            pltpu.SemaphoreType.DMA((slots_a,)),
            pltpu.SemaphoreType.DMA((slots_a,)),
            pltpu.SemaphoreType.DMA((n_grp,)),
            pltpu.SemaphoreType.DMA((n_grp,)),
            pltpu.SemaphoreType.DMA((OPERANDS,)),
        ],
        compiler_params=pltpu.CompilerParams(collective_id=0, has_side_effects=True),
        name="section",
    )(*arguments)
    store_next = RUNGE_CARRY * held_store + stepped
    fields_next = held_fields + RUNGE_ADVANCE * store_next
    return from_rows(fields_next), from_rows(store_next), energy.reshape(())


def solution(mesh):
    along = ("grp", "sub")
    placed = (
        P(None, None, along),
        P(None, None, along),
        P(None, along),
        P(None, None, along),
        P(None, along),
        P(along),
        P(along),
        P(along),
        P(None, along),
        P(None, along),
        P(),
        P(),
    )
    return jax.shard_map(
        local,
        mesh=mesh,
        in_specs=placed,
        out_specs=(P(None, None, along), P(None, None, along), P()),
        check_vma=False,
    )
```

profile of v0, /device:TPU:0, one launch (start us, length us, event | category | flops | bytes accessed | tf_op | source)
XLA Modules:
  0.0 21.5 jit_solution(3862478002258663796)
XLA Ops:
  0.6 18.3 %section.1 = (f32[280,128]{1,0:T(8,128)S(1)}, f32[280,128]{1,0:T(8,128)S(1)}, f32[280,128]{1,0:T(8,128)S(1)}, f32[1,1]{1,0:T(1,128)}) custom-call(f32[280,128]{1,0:T(8,128)} %bitcast.33, f32[280,128]{1,0:T(8,128)} %bitcast.34, f32[9,256]{1,0:T(8,128)} %refs_2_.1, f32[3,4,256]{2,1,0:T(4,128)} %bitcast.37, f32[4,256]{1,0:T(4,128)} %refs_4_.1, ...), custom_call_target="tpu_custom_call" | custom-call | tf_op jit(solution)/shard_map/section/pallas_call | solution.py:509
  19.0 0.7 %multiply_add_fusion = (f32[280,128]{1,0:T(8,128)}, f32[280,128]{1,0:T(8,128)}) fusion(f32[280,128]{1,0:T(8,128)S(1)} %get-tuple-element.7, f32[280,128]{1,0:T(8,128)S(1)} %get-tuple-element.9, f32[280,128]{1,0:T(8,128)S(1)} %get-tuple-element.8), kind=kLoop, calls=%fused_computation | loop fusion | flops 143360 | bytes 716800 | tf_op jit(solution)/shard_map/add | solution.py:543
where the time goes:
time: 21.6 us; the launch traced here: 21.5 us
  Pallas kernels  18.3 us (85%)
  between operations  2.41 us (11%)
  other arithmetic  0.75 us (3%)
    pallas_call x1, Pallas kernels, local(): pl.pallas_call(functools.partial(kernel, n_grp, n_sub, direct), out_shape...  18.3 us
    add x1, other arithmetic, local(): fields_next = held_fields + RUNGE_ADVANCE * store_next  0.75 us

commit v1 on v0

--- a/solution.py
+++ b/solution.py
@@ -167,7 +167,6 @@
 
     g = lax.axis_index("grp")
     s = lax.axis_index("sub")
-    inbox[...] = jnp.zeros_like(inbox)
 
     def sub_peer(k):
         return lax.rem(s + k, n_sub)
@@ -175,6 +174,12 @@
     def grp_peer(k):
         return lax.rem(g + k, n_grp)
 
+    inbox[...] = jnp.zeros_like(inbox)
+    for i in early:
+        loads[i].start()
+    for i in range(OPERANDS):
+        if i not in early:
+            loads[i].start()
     barrier = pltpu.get_barrier_semaphore()
     greeted = 0
     for kg in range(n_grp):
@@ -185,11 +190,6 @@
                 barrier, inc=1, device_id=(grp_peer(kg), sub_peer(ks)), device_id_type=MESH
             )
             greeted += 1
-    for i in early:
-        loads[i].start()
-    for i in range(OPERANDS):
-        if i not in early:
-            loads[i].start()
     for i in early:
         loads[i].wait()
 
@@ -443,8 +443,7 @@
         )
         column_peers = [(grp_peer(k), (grp_peer(k), s)) for k in range(1, n_grp)]
         total = spread_rows(energy_mid, energy_b, esend_b, erecv_b, g, column_peers)
-    divisor = elements * n_grp * n_sub * VOLUME_NODES
-    energy_out[0, 0] = jnp.sum(total) / divisor
+    energy_out[...] = total
 
     each_sub(sub_copy, lambda copy: copy.wait_send())
 
@@ -455,6 +454,13 @@
     @pl.when(g < n_grp - 1)
     def _():
         grp_copy(True).wait_send()
+
+
+def finish(divisor, fields, store, stepped, energy, fields_next, store_next, energy_mean):
+    energy_mean[...] = jnp.sum(energy[...], axis=1, keepdims=True) / divisor
+    moved = RUNGE_CARRY * store[...] + stepped[...]
+    store_next[...] = moved
+    fields_next[...] = fields[...] + RUNGE_ADVANCE * moved
 
 
 def local(
@@ -512,10 +518,10 @@
             pltpu.VMEM(flat, f32),
             pltpu.VMEM(flat, f32),
             pltpu.VMEM(flat, f32),
-            jax.ShapeDtypeStruct((1, 1), f32),
+            pltpu.VMEM((1, 128), f32),
         ),
         in_specs=[pl.BlockSpec(memory_space=pl.ANY)] * OPERANDS,
-        out_specs=(vmem, vmem, vmem, pl.BlockSpec(memory_space=pltpu.SMEM)),
+        out_specs=(vmem, vmem, vmem, vmem),
         scratch_shapes=[pltpu.VMEM(value.shape, value.dtype) for value in arguments[2:]]
         + [
             pltpu.VMEM((NODE_PAD, 4 * elements), f32),
@@ -539,8 +545,21 @@
         compiler_params=pltpu.CompilerParams(collective_id=0, has_side_effects=True),
         name="section",
     )(*arguments)
-    store_next = RUNGE_CARRY * held_store + stepped
-    fields_next = held_fields + RUNGE_ADVANCE * store_next
+    held = [
+        pltpu.with_memory_space_constraint(value, pltpu.VMEM)
+        for value in (held_fields, held_store, stepped, energy)
+    ]
+    fields_next, store_next, energy = pl.pallas_call(
+        functools.partial(finish, elements * n_grp * n_sub * VOLUME_NODES),
+        out_shape=(
+            jax.ShapeDtypeStruct(flat, f32),
+            jax.ShapeDtypeStruct(flat, f32),
+            jax.ShapeDtypeStruct((1, 1), f32),
+        ),
+        in_specs=[vmem] * 4,
+        out_specs=(vmem, vmem, vmem),
+        name="finish",
+    )(*held)
     return from_rows(fields_next), from_rows(store_next), energy.reshape(())
 
 

time: 21.6 us -> 19.2 us (0.89)
  between operations: 2.41 us -> 0.64 us
  other arithmetic: 0.75 us -> 0 us
    add x1 -> x0, other arithmetic: 0.75 us -> none  [local(): fields_next = held_fields + RUNGE_ADVANCE * store_next]
    pallas_call x0 -> x1, Pallas kernels: none -> 0.73 us  [local(): pl.pallas_call(functools.partial(finish, elements * n_grp * n_sub * VOLUM...]
    pallas_call x1, Pallas kernels: 18.3 us -> 17.7 us  [local(): pl.pallas_call(functools.partial(kernel, n_grp, n_sub, direct), out_shape...]
where the time goes in v1:
time: 19.2 us; the launch traced here: 19 us
  Pallas kernels  18.4 us (96%)
  between operations  0.64 us (3%)
    pallas_call x1, Pallas kernels, local(): pl.pallas_call(functools.partial(kernel, n_grp, n_sub, direct), out_shape...  17.7 us
    pallas_call x1, Pallas kernels, local(): pl.pallas_call(functools.partial(finish, elements * n_grp * n_sub * VOLUM...  0.73 us

profile of v1, /device:TPU:0, one launch (start us, length us, event | category | flops | bytes accessed | tf_op | source)
XLA Modules:
  0.0 19.0 jit_solution(15984511711876427523)
XLA Ops:
  0.6 17.7 %section.1 = (f32[280,128]{1,0:T(8,128)S(1)}, f32[280,128]{1,0:T(8,128)S(1)}, f32[280,128]{1,0:T(8,128)S(1)}, f32[1,128]{1,0:T(1,128)S(1)}) custom-call(f32[280,128]{1,0:T(8,128)} %bitcast.33, f32[280,128]{1,0:T(8,128)} %bitcast.34, f32[9,256]{1,0:T(8,128)} %refs_2_.1, f32[3,4,256]{2,1,0:T(4,128)} %bitcast.35, f32[4,256]{1,0:T(4,128)} %refs_4_.1, ...), custom_call_target="tpu_custom_call" | custom-call | tf_op jit(solution)/shard_map/section/pallas_call | solution.py:515
  18.3 0.7 %finish.1 = (f32[280,128]{1,0:T(8,128)}, f32[280,128]{1,0:T(8,128)}, f32[1,1]{1,0:T(1,128)}) custom-call(f32[280,128]{1,0:T(8,128)S(1)} %get-tuple-element.10.fields, f32[280,128]{1,0:T(8,128)S(1)} %get-tuple-element.11.store, f32[280,128]{1,0:T(8,128)S(1)} %get-tuple-element.12.stepped, f32[1,128]{1,0:T(1,128)S(1)} %get-tuple-element.13.energy), custom_call_target="tpu_custom_call" | custom-call | tf_op jit(solution)/shard_map/finish/pallas_call | solution.py:552

commit v2 on v1

v2 whole, which is shorter than its diff:
```python
import functools

import jax
import jax.numpy as jnp
import numpy as np
from jax import lax
from jax.experimental import pallas as pl
from jax.experimental.pallas import tpu as pltpu
from jax.sharding import PartitionSpec as P

VOLUME_NODES = 35
FACE_NODES = 15
NODE_PAD = 48
SLOPE_PAD = 40
ROWS = 64
TURN_COLS = 768

RUNGE_CARRY = -567301805773.0 / 1357537059087.0
RUNGE_ADVANCE = 5161836677717.0 / 13612068292357.0
TIME_STEP = 0.02
OPERANDS = 14
MESH = pl.DeviceIdType.MESH


def node_tables():
    volume_list = [
        (a, b, c, 4 - a - b - c) for a in range(5) for b in range(5 - a) for c in range(5 - a - b)
    ]
    triples = [(a, b, 4 - a - b) for a in range(5) for b in range(5 - a)]
    face_index = np.zeros((4, 15), np.int32)
    for facet in range(4):
        others = [corner for corner in range(4) if corner != facet]
        for node_pos in range(15):
            corners = [0, 0, 0, 0]
            for place_pos in range(3):
                corners[others[place_pos]] = triples[node_pos][place_pos]
            face_index[facet, node_pos] = volume_list.index(tuple(corners))
    vertex_orders = [(0, 1, 2), (1, 2, 0), (2, 0, 1), (0, 2, 1), (2, 1, 0), (1, 0, 2)]
    turn_index = np.zeros((6, 15), np.int32)
    for option in range(6):
        q = vertex_orders[option]
        for node_pos in range(15):
            t = triples[node_pos]
            turn_index[option, node_pos] = triples.index((t[q[0]], t[q[1]], t[q[2]]))
    return face_index, turn_index


def constant_tables():
    face_index, turn_index = node_tables()
    pick = np.zeros((ROWS, 128), np.float32)
    turn = np.zeros((ROWS, TURN_COLS), np.float32)
    spread = np.zeros((ROWS, 128 + 24 * 16), np.float32)
    for f in range(4):
        for j in range(15):
            pick[f * 16 + j, face_index[f, j]] = 1.0
            spread[f * 15 + j, f * 16 + j] = 1.0
            for o in range(6):
                spread[f * 15 + j, 128 + (f * 6 + o) * 16 + turn_index[o, j]] = 1.0
    for part in range(2):
        for o in range(6):
            for c in range(4):
                for j in range(15):
                    col = part * 384 + o * 64 + c * 16 + turn_index[o, j]
                    turn[c * 16 + j, col] = 1.0
    later = np.concatenate([turn, spread], axis=1)
    return jnp.asarray(pick, jnp.bfloat16), jnp.asarray(later, jnp.bfloat16)


def split(value):
    high = value.astype(jnp.bfloat16)
    low = (value - high.astype(jnp.float32)).astype(jnp.bfloat16)
    return high, low


def dot(left, right):
    return jnp.dot(left, right, preferred_element_type=jnp.float32)


def dot3(left, right):
    (lh, ll), (rh, rl) = left, right
    return dot(lh, rh) + (dot(lh, rl) + dot(ll, rh))


def flat_row(ref_rows):
    return jnp.concatenate(ref_rows, axis=1)


def split3(value):
    high, rest = split(value)
    low = value - high.astype(jnp.float32) - rest.astype(jnp.float32)
    return high, rest, low.astype(jnp.bfloat16)


def kernel(
    n_grp,
    n_sub,
    direct,
    *refs,
):
    operands, rest = refs[:OPERANDS], refs[OPERANDS:]
    results, rest = rest[:3], rest[3:]
    copies, rest = rest[:OPERANDS], rest[OPERANDS:]
    body(n_grp, n_sub, direct, operands, copies, *results, *rest)


def body(
    n_grp,
    n_sub,
    direct,
    operands,
    copies,
    fields_out,
    store_out,
    energy_out,
    fpad,
    dpad,
    lpad,
    outbox,
    inbox,
    moved,
    stored,
    energy_row,
    energy_mid,
    energy_a,
    energy_b,
    trace_sem,
    energy_sem,
    load_sem,
):
    (
        fields,
        store,
        metric,
        normals,
        face_scale,
        damping,
        mask,
        level,
        source,
        orient,
        derivative,
        lift,
        pick_table,
        table,
    ) = copies
    loads = [
        pltpu.make_async_copy(operands[i], copies[i], load_sem.at[i]) for i in range(OPERANDS)
    ]
    early = (0, 8, 12)
    elements = face_scale.shape[1]
    tiles = elements // 128
    faces = 4 * elements
    half = elements // 16
    n_blocks = n_sub + 2

    def node_rows(c, t):
        return pl.ds(t * 4 + c, VOLUME_NODES, stride=4 * tiles)

    def read(ref, c):
        return jnp.concatenate([ref[node_rows(c, t), :] for t in range(tiles)], axis=1)

    def write(ref, c, value):
        for t in range(tiles):
            ref[node_rows(c, t), :] = value[:, t * 128 : (t + 1) * 128]

    g = lax.axis_index("grp")
    s = lax.axis_index("sub")

    def sub_peer(k):
        return lax.rem(s + k, n_sub)

    def grp_peer(k):
        return lax.rem(g + k, n_grp)

    inbox[...] = jnp.zeros_like(inbox)
    for i in early:
        loads[i].start()
    for i in range(OPERANDS):
        if i not in early:
            loads[i].start()
    barrier = pltpu.get_barrier_semaphore()
    for k in range(1, n_sub):
        pl.semaphore_signal(barrier, inc=1, device_id=(g, sub_peer(k)), device_id_type=MESH)
    for k in range(1, n_grp):
        pl.semaphore_signal(barrier, inc=1, device_id=(grp_peer(k), s), device_id_type=MESH)
    greeted = n_sub + n_grp - 2
    for i in early:
        loads[i].wait()

    fpad[VOLUME_NODES:, :] = jnp.zeros((NODE_PAD - VOLUME_NODES, faces), jnp.float32)
    for c in range(4):
        fpad[0:VOLUME_NODES, c * elements : (c + 1) * elements] = read(fields, c)
    field_parts = split(fpad[...])
    pick = pick_table[:, 0:NODE_PAD]

    def by_face(value):
        return jnp.concatenate(
            [
                jnp.concatenate(
                    [
                        value[f * 16 : (f + 1) * 16, c * elements : (c + 1) * elements]
                        for c in range(4)
                    ],
                    axis=0,
                )
                for f in range(4)
            ],
            axis=1,
        )

    inner_high = by_face(dot(pick, field_parts[0]))
    inner_low = by_face(dot(pick, field_parts[1]))
    codes = flat_row([source[f : f + 1, :] for f in range(4)])
    high_b = inner_high.astype(jnp.bfloat16)
    low_b = inner_low.astype(jnp.bfloat16)

    def slots_hot(part):
        row = lax.broadcasted_iota(jnp.int32, (n_blocks * half, faces), 0)
        slot = (row // half) * (2 * half) + part * half + row % half
        return jnp.where(slot == codes - faces, 1.0, 0.0).astype(jnp.bfloat16)

    hot = [slots_hot(0), slots_hot(1)]
    nothing = jnp.zeros_like(high_b)
    packed = None
    for part in range(2):
        for value in (high_b, low_b):
            weights = jnp.concatenate([value, nothing] if part == 0 else [nothing, value], axis=0)
            term = lax.dot_general(
                hot[part], weights, (((1,), (1,)), ((), ())), preferred_element_type=jnp.float32
            )
            packed = term if packed is None else packed + term
    outbox[...] = packed

    pl.semaphore_wait(barrier, greeted)

    def block(ref, at):
        return ref.at[pl.ds(pl.multiple_of(at * half, half), half)]

    def trace_copy(source_block, landing_block, device):
        return pltpu.make_async_remote_copy(
            src_ref=block(outbox, source_block),
            dst_ref=block(inbox, landing_block),
            send_sem=trace_sem.at[0],
            recv_sem=trace_sem.at[1],
            device_id=device,
            device_id_type=MESH,
        )

    def trace_total(blocks):
        return pltpu.make_async_remote_copy(
            src_ref=outbox.at[pl.ds(0, blocks * half)],
            dst_ref=inbox.at[pl.ds(0, blocks * half)],
            send_sem=trace_sem.at[0],
            recv_sem=trace_sem.at[1],
            device_id=(g, sub_peer(1)),
            device_id_type=MESH,
        )

    inner = jnp.logical_and(g > 0, g < n_grp - 1)

    def each_total(act):
        @pl.when(inner)
        def _():
            act(trace_total(n_sub + 1))

        @pl.when(jnp.logical_not(inner))
        def _():
            act(trace_total(n_sub))

    for k in range(1, n_sub):
        trace_copy(sub_peer(k), s, (g, sub_peer(k))).start()

    @pl.when(g > 0)
    def _():
        trace_copy(n_sub, n_sub + 1, (jnp.maximum(g - 1, 0), s)).start()

    @pl.when(g < n_grp - 1)
    def _():
        trace_copy(n_sub + 1, n_sub, (jnp.minimum(g + 1, n_grp - 1), s)).start()

    for i in range(OPERANDS):
        if i not in early:
            loads[i].wait()
    growth = jnp.exp2(level[...].astype(jnp.float32))
    absorb = damping[...] * mask[...].astype(jnp.float32)
    dpad[...] = jnp.zeros_like(dpad)
    for d in range(3):
        dpad[d * SLOPE_PAD : d * SLOPE_PAD + VOLUME_NODES, 0:VOLUME_NODES] = derivative[d]
    slopes = dot3(split(dpad[...]), field_parts)

    def slope(d, c):
        return slopes[
            d * SLOPE_PAD : (d + 1) * SLOPE_PAD, c * elements : (c + 1) * elements
        ]

    def field(c):
        return fpad[0:VOLUME_NODES, c * elements : (c + 1) * elements]

    lpad[...] = jnp.zeros_like(lpad)
    lpad[0:VOLUME_NODES, 0:60] = lift[...]
    spread = table[:, TURN_COLS : TURN_COLS + ROWS]
    turned_spread = table[:, TURN_COLS + 128 : TURN_COLS + 128 + 24 * 16]
    lift_split = split(lpad[...])
    lift_parts = tuple(dot(part, spread).astype(jnp.bfloat16) for part in lift_split)
    turned_lift = tuple(dot(part, turned_spread).astype(jnp.bfloat16) for part in lift_split)

    stacked = jnp.concatenate([high_b, low_b], axis=0)
    gathered = None
    for f in range(4):
        row = lax.broadcasted_iota(jnp.int32, (elements, faces), 0) + f * elements
        chosen = jnp.where(row == codes, 1.0, 0.0).astype(jnp.bfloat16)
        term = dot(stacked[:, f * elements : (f + 1) * elements], chosen)
        gathered = term if gathered is None else gathered + term

    turns = flat_row([orient[f : f + 1, :] for f in range(4)])
    pieces = []
    for part in range(2):
        value = gathered[part * ROWS : (part + 1) * ROWS]
        for o in range(6):
            pieces.append(jnp.where(turns == o, value, 0.0).astype(jnp.bfloat16))
    outside = dot(table[:, 0:TURN_COLS], jnp.concatenate(pieces, axis=0))
    inside = inner_high + inner_low

    wall = codes < 0
    normal = [
        flat_row([normals[x, f : f + 1, :] for f in range(4)]) for x in range(3)
    ]
    weight = 0.5 * flat_row([face_scale[f : f + 1, :] * growth for f in range(4)])
    press = jnp.where(wall, 0.0, inside[0:16] - outside[0:16])
    normal_in = None
    for x in range(3):
        term = normal[x] * inside[16 * (x + 1) : 16 * (x + 2)]
        normal_in = term if normal_in is None else normal_in + term
    normal_jump = None
    for x in range(3):
        rows = slice(16 * (x + 1), 16 * (x + 2))
        jump = jnp.where(wall, 2.0 * normal[x] * normal_in, inside[rows] - outside[rows])
        term = normal[x] * jump
        normal_jump = term if normal_jump is None else normal_jump + term
    flux_press = weight * (normal_jump - press)
    fluxes = [flux_press] + [-normal[x] * flux_press for x in range(3)]
    flux = jnp.concatenate(
        [
            jnp.concatenate(
                [flux_c[:, f * elements : (f + 1) * elements] for f in range(4)], axis=0
            )
            for flux_c in fluxes
        ],
        axis=1,
    )
    lifted = dot3(lift_parts, split(flux))
    scaled = metric[...] * growth
    for c in range(4):
        total = None
        for x in range(3) if c == 0 else (c - 1,):
            for y in range(3):
                term = scaled[3 * x + y : 3 * x + y + 1, :] * slope(y, x + 1 if c == 0 else 0)
                total = term if total is None else total + term
        lift_c = lifted[:, c * elements : (c + 1) * elements]
        change = lift_c - total - absorb * fpad[0:SLOPE_PAD, c * elements : (c + 1) * elements]
        stepped = TIME_STEP * change[0:VOLUME_NODES] + RUNGE_CARRY * read(store, c)
        stored[c, 0:VOLUME_NODES, :] = stepped
        moved[c, 0:VOLUME_NODES, :] = field(c) + RUNGE_ADVANCE * stepped
        for ref in (stored, moved):
            ref[c, VOLUME_NODES:, :] = jnp.zeros((SLOPE_PAD - VOLUME_NODES, elements), jnp.float32)

    face_row = lax.broadcasted_iota(jnp.int32, (1, faces), 1) // elements
    kinds = (face_row * 6 + turns).astype(jnp.bfloat16)
    meta_rows = []
    for value in normal + [TIME_STEP * weight]:
        meta_rows.extend(split3(value))
    meta = jnp.concatenate(
        [row.astype(jnp.float32) for row in meta_rows]
        + [kinds.astype(jnp.float32)]
        + [jnp.zeros((3, faces), jnp.float32)],
        axis=0,
    ).astype(jnp.bfloat16)
    slot_normal, slot_weight, slot_kind, slot_element = [], [], [], []
    for part in range(2):
        found = lax.dot_general(
            meta, hot[part], (((1,), (1,)), ((), ())), preferred_element_type=jnp.float32
        )
        rows = [
            found[3 * i : 3 * i + 1] + (found[3 * i + 1 : 3 * i + 2] + found[3 * i + 2 : 3 * i + 3])
            for i in range(4)
        ]
        slot_normal.append(rows[:3])
        slot_weight.append(rows[3])
        slot_kind.append(found[12:13].astype(jnp.int32))
        at_element = hot[part][:, 0:elements]
        for f in range(1, 4):
            at_element = at_element + hot[part][:, f * elements : (f + 1) * elements]
        slot_element.append(at_element)

    each_total(lambda copy: copy.wait_recv())

    arrived = inbox[...].T
    landed = None
    for part in range(2):
        value = arrived[part * ROWS : (part + 1) * ROWS]
        outer = value[0:16]
        for x in range(3):
            outer = outer - slot_normal[part][x] * value[16 * (x + 1) : 16 * (x + 2)]
        outer_parts = split(slot_weight[part] * outer)
        spread_parts = [
            jnp.concatenate(
                [
                    jnp.where(slot_kind[part] == kind, piece, jnp.zeros_like(piece))
                    for kind in range(24)
                ],
                axis=0,
            )
            for piece in outer_parts
        ]
        press_lift = dot3(turned_lift, spread_parts)
        slot_lift = jnp.concatenate(
            [press_lift] + [-slot_normal[part][x] * press_lift for x in range(3)], axis=0
        )
        slot_parts = jnp.concatenate(split(slot_lift), axis=0)
        term = dot(slot_parts, slot_element[part])
        landed = term if landed is None else landed + term
    remote = landed[0 : 4 * SLOPE_PAD] + landed[4 * SLOPE_PAD :]
    squares = None
    for c in range(4):
        remote_c = remote[c * SLOPE_PAD : (c + 1) * SLOPE_PAD]
        moved_c = moved[c] + RUNGE_ADVANCE * remote_c
        moved[c] = moved_c
        stored[c] = stored[c] + remote_c
        squares = moved_c * moved_c if squares is None else squares + moved_c * moved_c
    weighted = absorb * jnp.sum(squares, axis=0, keepdims=True)
    partial = weighted[:, 0:128]
    for at in range(128, elements, 128):
        partial = partial + weighted[:, at : at + 128]
    energy_row[...] = partial

    def write_results():
        for c in range(4):
            write(fields_out, c, moved[c, 0:VOLUME_NODES, :])
            write(store_out, c, stored[c, 0:VOLUME_NODES, :])

    def spread_rows(source_row, landing, stage, mine, peers, after_sends=lambda: None):
        def copy(source, target, device):
            return pltpu.make_async_remote_copy(
                src_ref=source,
                dst_ref=target,
                send_sem=energy_sem.at[2 * stage],
                recv_sem=energy_sem.at[2 * stage + 1],
                device_id=device,
                device_id_type=MESH,
            )

        for device in peers:
            copy(source_row, landing.at[mine], device).start()
        landing[mine] = source_row[...]
        after_sends()
        others = landing.at[pl.ds(0, len(peers))]
        total = copy(others, others, peers[0])
        total.wait_recv()
        total.wait_send()
        return jnp.sum(landing[...], axis=0)

    if direct:
        everyone = [
            (grp_peer(kg), sub_peer(ks))
            for kg in range(n_grp)
            for ks in range(n_sub)
            if (kg, ks) != (0, 0)
        ]
        total = spread_rows(energy_row, energy_a, 0, g * n_sub + s, everyone, write_results)
    else:
        row_peers = [(g, sub_peer(k)) for k in range(1, n_sub)]
        energy_mid[...] = spread_rows(energy_row, energy_a, 0, s, row_peers, write_results)
        column_peers = [(grp_peer(k), s) for k in range(1, n_grp)]
        total = spread_rows(energy_mid, energy_b, 1, g, column_peers)
    energy_out[...] = total
    each_total(lambda copy: copy.wait_send())


def finish(divisor, fields, store, energy, fields_next, store_next, energy_mean, mean, sem):
    copies = [
        pltpu.make_async_copy(source, target, sem.at[i])
        for i, (source, target) in enumerate(
            [(fields, fields_next), (store, store_next), (mean, energy_mean)]
        )
    ]
    copies[0].start()
    copies[1].start()
    mean[...] = jnp.sum(energy[...], axis=1, keepdims=True) / divisor
    copies[2].start()
    for copy in copies:
        copy.wait()


def local(
    fields,
    section_store,
    metric_terms,
    normals,
    face_scale,
    damping,
    absorb_mask,
    refine_level,
    face_source,
    orientation,
    derivative,
    lift_matrix,
):
    elements = fields.shape[2]
    n_grp, n_sub = lax.axis_size("grp"), lax.axis_size("sub")
    direct = n_grp * n_sub <= 64
    n_blocks = n_sub + 2
    half = elements // 16
    slots_a = n_grp * n_sub if direct else n_sub
    row = lambda value: value.reshape(1, elements)
    vmem = pl.BlockSpec(memory_space=pltpu.VMEM)
    anywhere = pl.BlockSpec(memory_space=pl.ANY)
    f32 = jnp.float32
    tiles = elements // 128

    def to_rows(value):
        value = value.transpose(1, 0, 2).reshape(VOLUME_NODES, 4, tiles, 128)
        return value.transpose(0, 2, 1, 3).reshape(VOLUME_NODES * tiles * 4, 128)

    def from_rows(value):
        value = value.reshape(VOLUME_NODES, tiles, 4, 128).transpose(0, 2, 1, 3)
        return value.reshape(VOLUME_NODES, 4, elements).transpose(1, 0, 2)

    flat = (VOLUME_NODES * tiles * 4, 128)
    arguments = (
        to_rows(fields),
        to_rows(section_store),
        metric_terms,
        normals.transpose(1, 0, 2),
        face_scale,
        row(damping),
        row(absorb_mask),
        row(refine_level),
        face_source,
        orientation,
        derivative,
        lift_matrix,
        *constant_tables(),
    )
    held = pl.pallas_call(
        functools.partial(kernel, n_grp, n_sub, direct),
        out_shape=(pltpu.VMEM(flat, f32), pltpu.VMEM(flat, f32), pltpu.VMEM((1, 128), f32)),
        in_specs=[anywhere] * OPERANDS,
        out_specs=(vmem,) * 3,
        scratch_shapes=[pltpu.VMEM(value.shape, value.dtype) for value in arguments]
        + [
            pltpu.VMEM((NODE_PAD, 4 * elements), f32),
            pltpu.VMEM((3 * SLOPE_PAD, NODE_PAD), f32),
            pltpu.VMEM((SLOPE_PAD, ROWS), f32),
            pltpu.VMEM((n_blocks * half, 2 * ROWS), f32),
            pltpu.VMEM((n_blocks * half, 2 * ROWS), f32),
            pltpu.VMEM((4, SLOPE_PAD, elements), f32),
            pltpu.VMEM((4, SLOPE_PAD, elements), f32),
            pltpu.VMEM((1, 128), f32),
            pltpu.VMEM((1, 128), f32),
            pltpu.VMEM((slots_a, 1, 128), f32),
            pltpu.VMEM((n_grp, 1, 128), f32),
            pltpu.SemaphoreType.DMA((2,)),
            pltpu.SemaphoreType.DMA((2 if direct else 4,)),
            pltpu.SemaphoreType.DMA((OPERANDS,)),
        ],
        compiler_params=pltpu.CompilerParams(collective_id=0, has_side_effects=True),
        name="section",
    )(*arguments)
    held = [pltpu.with_memory_space_constraint(value, pltpu.VMEM) for value in held]
    fields_next, store_next, energy = pl.pallas_call(
        functools.partial(finish, elements * n_grp * n_sub * VOLUME_NODES),
        out_shape=(
            jax.ShapeDtypeStruct(flat, f32),
            jax.ShapeDtypeStruct(flat, f32),
            jax.ShapeDtypeStruct((1, 1), f32),
        ),
        in_specs=[vmem] * 3,
        out_specs=(anywhere,) * 3,
        scratch_shapes=[pltpu.VMEM((1, 1), f32), pltpu.SemaphoreType.DMA((3,))],
        name="finish",
    )(*held)
    return from_rows(fields_next), from_rows(store_next), energy.reshape(())


def solution(mesh):
    along = ("grp", "sub")
    placed = (
        P(None, None, along),
        P(None, None, along),
        P(None, along),
        P(None, None, along),
        P(None, along),
        P(along),
        P(along),
        P(along),
        P(None, along),
        P(None, along),
        P(),
        P(),
    )
    return jax.shard_map(
        local,
        mesh=mesh,
        in_specs=placed,
        out_specs=(P(None, None, along), P(None, None, along), P()),
        check_vma=False,
    )
```

time: 19.2 us -> 17.8 us (0.927)
  Pallas kernels: 18.4 us -> 17 us
    pallas_call x1, Pallas kernels: 17.7 us -> 16.3 us  [local(): pl.pallas_call(functools.partial(kernel, n_grp, n_sub, direct), out_shape...]
where the time goes in v2:
time: 17.8 us; the launch traced here: 17.7 us
  Pallas kernels  17 us (96%)
  between operations  0.64 us (4%)
    pallas_call x1, Pallas kernels, local(): pl.pallas_call(functools.partial(kernel, n_grp, n_sub, direct), out_shape...  16.3 us
    pallas_call x1, Pallas kernels, local(): pl.pallas_call(functools.partial(finish, elements * n_grp * n_sub * VOLUM...  0.74 us

profile of v2, /device:TPU:0, one launch (start us, length us, event | category | flops | bytes accessed | tf_op | source)
XLA Modules:
  0.0 17.7 jit_solution(15630673724634646904)
XLA Ops:
  0.6 16.3 %section.1 = (f32[280,128]{1,0:T(8,128)S(1)}, f32[280,128]{1,0:T(8,128)S(1)}, f32[1,128]{1,0:T(1,128)S(1)}) custom-call(f32[280,128]{1,0:T(8,128)} %bitcast.33, f32[280,128]{1,0:T(8,128)} %bitcast.34, f32[9,256]{1,0:T(8,128)} %refs_2_.1, f32[3,4,256]{2,1,0:T(4,128)} %bitcast.35, f32[4,256]{1,0:T(4,128)} %refs_4_.1, f32[1,256]{1,0:T(1,128)} %bitcast.36, ...), custom_call_target="tpu_custom_call" | custom-call | tf_op jit(solution)/shard_map/section/pallas_call | solution.py:544
  17.0 0.7 %finish.1 = (f32[280,128]{1,0:T(8,128)}, f32[280,128]{1,0:T(8,128)}, f32[1,1]{1,0:T(1,128)}) custom-call(f32[280,128]{1,0:T(8,128)S(1)} %get-tuple-element.9.fields, f32[280,128]{1,0:T(8,128)S(1)} %get-tuple-element.10.store, f32[1,128]{1,0:T(1,128)S(1)} %get-tuple-element.11.energy), custom_call_target="tpu_custom_call" | custom-call | tf_op jit(solution)/shard_map/finish/pallas_call | solution.py:570

commit v3 on v2

--- a/solution.py
+++ b/solution.py
@@ -119,6 +119,7 @@
     inbox,
     moved,
     stored,
+    kind_mask,
     energy_row,
     energy_mid,
     energy_a,
@@ -173,16 +174,16 @@
         return lax.rem(g + k, n_grp)
 
     inbox[...] = jnp.zeros_like(inbox)
+    barrier = pltpu.get_barrier_semaphore()
+    for k in range(1, n_sub):
+        pl.semaphore_signal(barrier, inc=1, device_id=(g, sub_peer(k)), device_id_type=MESH)
+    for k in range(1, n_grp):
+        pl.semaphore_signal(barrier, inc=1, device_id=(grp_peer(k), s), device_id_type=MESH)
     for i in early:
         loads[i].start()
     for i in range(OPERANDS):
         if i not in early:
             loads[i].start()
-    barrier = pltpu.get_barrier_semaphore()
-    for k in range(1, n_sub):
-        pl.semaphore_signal(barrier, inc=1, device_id=(g, sub_peer(k)), device_id_type=MESH)
-    for k in range(1, n_grp):
-        pl.semaphore_signal(barrier, inc=1, device_id=(grp_peer(k), s), device_id_type=MESH)
     greeted = n_sub + n_grp - 2
     for i in early:
         loads[i].wait()
@@ -267,8 +268,9 @@
         def _():
             act(trace_total(n_sub))
 
-    for k in range(1, n_sub):
-        trace_copy(sub_peer(k), s, (g, sub_peer(k))).start()
+    for k in range(n_sub - 2, -1, -1):
+        peer = jnp.where(k < s, k, k + 1)
+        trace_copy(peer, s, (g, peer)).start()
 
     @pl.when(g > 0)
     def _():
@@ -375,7 +377,7 @@
         + [jnp.zeros((3, faces), jnp.float32)],
         axis=0,
     ).astype(jnp.bfloat16)
-    slot_normal, slot_weight, slot_kind, slot_element = [], [], [], []
+    slot_normal, slot_weight, slot_element = [], [], []
     for part in range(2):
         found = lax.dot_general(
             meta, hot[part], (((1,), (1,)), ((), ())), preferred_element_type=jnp.float32
@@ -386,7 +388,11 @@
         ]
         slot_normal.append(rows[:3])
         slot_weight.append(rows[3])
-        slot_kind.append(found[12:13].astype(jnp.int32))
+        kind = jnp.broadcast_to(found[12:13], (16, n_blocks * half))
+        for at in range(24):
+            kind_mask[part, at * 16 : (at + 1) * 16, :] = jnp.where(
+                kind == at, 1.0, 0.0
+            ).astype(jnp.bfloat16)
         at_element = hot[part][:, 0:elements]
         for f in range(1, 4):
             at_element = at_element + hot[part][:, f * elements : (f + 1) * elements]
@@ -403,14 +409,7 @@
             outer = outer - slot_normal[part][x] * value[16 * (x + 1) : 16 * (x + 2)]
         outer_parts = split(slot_weight[part] * outer)
         spread_parts = [
-            jnp.concatenate(
-                [
-                    jnp.where(slot_kind[part] == kind, piece, jnp.zeros_like(piece))
-                    for kind in range(24)
-                ],
-                axis=0,
-            )
-            for piece in outer_parts
+            jnp.concatenate([piece] * 24, axis=0) * kind_mask[part] for piece in outer_parts
         ]
         press_lift = dot3(turned_lift, spread_parts)
         slot_lift = jnp.concatenate(
@@ -450,27 +449,26 @@
             )
 
         for device in peers:
-            copy(source_row, landing.at[mine], device).start()
+
+            @pl.when(jnp.logical_or(device[0] != g, device[1] != s))
+            def _():
+                copy(source_row, landing.at[mine], device).start()
+
         landing[mine] = source_row[...]
         after_sends()
-        others = landing.at[pl.ds(0, len(peers))]
-        total = copy(others, others, peers[0])
+        others = landing.at[pl.ds(0, len(peers) - 1)]
+        total = copy(others, others, (g, sub_peer(1)))
         total.wait_recv()
         total.wait_send()
         return jnp.sum(landing[...], axis=0)
 
     if direct:
-        everyone = [
-            (grp_peer(kg), sub_peer(ks))
-            for kg in range(n_grp)
-            for ks in range(n_sub)
-            if (kg, ks) != (0, 0)
-        ]
+        everyone = [(kg, ks) for ks in range(n_sub) for kg in range(n_grp)]
         total = spread_rows(energy_row, energy_a, 0, g * n_sub + s, everyone, write_results)
     else:
-        row_peers = [(g, sub_peer(k)) for k in range(1, n_sub)]
+        row_peers = [(g, k) for k in range(n_sub)]
         energy_mid[...] = spread_rows(energy_row, energy_a, 0, s, row_peers, write_results)
-        column_peers = [(grp_peer(k), s) for k in range(1, n_grp)]
+        column_peers = [(k, s) for k in range(n_grp)]
         total = spread_rows(energy_mid, energy_b, 1, g, column_peers)
     energy_out[...] = total
     each_total(lambda copy: copy.wait_send())
@@ -555,6 +553,7 @@
             pltpu.VMEM((n_blocks * half, 2 * ROWS), f32),
             pltpu.VMEM((4, SLOPE_PAD, elements), f32),
             pltpu.VMEM((4, SLOPE_PAD, elements), f32),
+            pltpu.VMEM((2, 24 * 16, n_blocks * half), jnp.bfloat16),
             pltpu.VMEM((1, 128), f32),
             pltpu.VMEM((1, 128), f32),
             pltpu.VMEM((slots_a, 1, 128), f32),

time: 17.8 us -> 17.3 us (0.972)
  Pallas kernels: 17 us -> 16.5 us
    pallas_call x1, Pallas kernels: 16.3 us -> 15.7 us  [local(): pl.pallas_call(functools.partial(kernel, n_grp, n_sub, direct), out_shape...]
where the time goes in v3:
time: 17.3 us; the launch traced here: 17.1 us
  Pallas kernels  16.5 us (95%)
  between operations  0.64 us (4%)
    pallas_call x1, Pallas kernels, local(): pl.pallas_call(functools.partial(kernel, n_grp, n_sub, direct), out_shape...  15.7 us
    pallas_call x1, Pallas kernels, local(): pl.pallas_call(functools.partial(finish, elements * n_grp * n_sub * VOLUM...  0.74 us

profile of v3, /device:TPU:0, one launch (start us, length us, event | category | flops | bytes accessed | tf_op | source)
XLA Modules:
  0.0 17.1 jit_solution(11077008904367395890)
XLA Ops:
  0.6 15.7 %section.1 = (f32[280,128]{1,0:T(8,128)S(1)}, f32[280,128]{1,0:T(8,128)S(1)}, f32[1,128]{1,0:T(1,128)S(1)}) custom-call(f32[280,128]{1,0:T(8,128)} %bitcast.33, f32[280,128]{1,0:T(8,128)} %bitcast.34, f32[9,256]{1,0:T(8,128)} %refs_2_.1, f32[3,4,256]{2,1,0:T(4,128)} %bitcast.35, f32[4,256]{1,0:T(4,128)} %refs_4_.1, f32[1,256]{1,0:T(1,128)} %bitcast.36, ...), custom_call_target="tpu_custom_call" | custom-call | tf_op jit(solution)/shard_map/section/pallas_call | solution.py:542
  16.4 0.7 %finish.1 = (f32[280,128]{1,0:T(8,128)}, f32[280,128]{1,0:T(8,128)}, f32[1,1]{1,0:T(1,128)}) custom-call(f32[280,128]{1,0:T(8,128)S(1)} %get-tuple-element.9.fields, f32[280,128]{1,0:T(8,128)S(1)} %get-tuple-element.10.store, f32[1,128]{1,0:T(1,128)S(1)} %get-tuple-element.11.energy), custom_call_target="tpu_custom_call" | custom-call | tf_op jit(solution)/shard_map/finish/pallas_call | solution.py:569
